TPU v7x, 64 devices: a 2x2x8 block of a 4x4x8 slice. The times are simulated.
64 devices in a mesh: dp: 8 (over x, y, core), sp: 8 (over z).
Axes of the slice: x: 2, y: 2, z: 8, core: 2. Of those that a mesh axis runs over, the one named last changes fastest.
The devices are a block of a 4x4x8 slice.
Arguments:
- q: bfloat16 [256, 64, 64], P('dp'), parts along dimension 0
- k: bfloat16 [256, 8192, 8, 64], P('dp', 'sp'), parts along dimension 0
- v: bfloat16 [256, 8192, 8, 64], P('dp', 'sp'), parts along dimension 0
Outputs:
- q: bfloat16 [256, 64, 64], P('dp'), parts along dimension 0
There are 8 independent parts. A program takes and returns all parts, laid end to end along the dimension named above; each array names one.
All inputs are finite; a program needn't handle non-finite values.
Results may differ from a plain program's by a relative error of at most 0.012.
Values are sent between devices in bfloat16 or wider.
A program may use at most 768 MiB of HBM per device.

v0:
```python
import jax
import jax.numpy as jnp
from jax import lax
from jax.sharding import PartitionSpec as P


def einsum(form, a, b):
    return jnp.einsum(form, a.astype(jnp.float32), b.astype(jnp.float32))


def part_of(q, k, v):
    grouped = q.reshape(q.shape[0], k.shape[2], -1, q.shape[2])
    scores = einsum("bgsd,bugd->bgsu", grouped, k) * q.shape[2] ** -0.5
    high = jnp.max(scores, -1, keepdims=True)
    weights = jnp.exp(scores - high)
    seen = einsum("bgsu,bugd->bgsd", weights.astype(jnp.bfloat16), v)
    return jnp.concatenate([seen, jnp.sum(weights, -1, keepdims=True), high], -1)


def together(parts):
    seen, total, high = parts[..., :-2], parts[..., -2:-1], parts[..., -1:]
    scale = jnp.exp(high - jnp.max(high, 0))
    return (jnp.sum(seen * scale, 0) / jnp.sum(total * scale, 0)).astype(jnp.bfloat16)


def solution(mesh):
    def step(q, k, v):
        return together(lax.all_gather(part_of(q, k, v), "sp")).reshape(q.shape)

    return jax.shard_map(
        step,
        mesh=mesh,
        in_specs=(P("dp", None, None), P("dp", "sp", None, None), P("dp", "sp", None, None)),
        out_specs=P("dp", None, None),
        check_vma=False,
    )
```

profile of v0, /device:TPU:21, one launch (start us, length us, event | category | flops | bytes accessed | tf_op | source)
XLA Modules:
  0.0 186.6 jit_solution(9621918656523116043)
XLA Ops:
  6.5 0.0 copy-start
  6.6 0.0 all-gather.3.cloned.1.call-start
  6.6 1.0 copy-done
  7.6 16.3 %multiply_reduce_fusion = (f32[32,8,8]{2,1,0:T(8,128)S(1)}, f32[32,8,8,1024]{3,2,1,0:T(8,128)}) fusion(bf16[32,1024,8,64]{1,3,2,0:T(8,128)(2,1)} %param.4, bf16[32,64,64]{2,1,0:T(8,128)(2,1)S(1)} %copy-done), kind=kOutput, calls=%fused_computation.7 | convolution fusion | flops 272627712 | bytes 42213376 | tf_op jit(solution)/shard_map/bgsd,bugd->bgsu/dot_general | solution.py:8
  23.9 0.0 copy-start.3
  23.9 4.7 %fusion.2 = f32[32,8,8]{2,1,0:T(8,128)S(1)} fusion(f32[32,8,8,1024]{3,2,1,0:T(8,128)} %get-tuple-element.8, f32[32,8,8]{2,1,0:T(8,128)S(1)} %get-tuple-element.7), kind=kLoop, calls=%fused_computation.8 | loop fusion | flops 6289408 | bytes 8404992 | tf_op jit(solution)/shard_map/reduce_sum | solution.py:17
  28.6 1.1 copy-done.3
  29.8 14.1 %fusion.4 = f32[32,8,8,64]{3,2,1,0:T(8,128)S(1)} fusion(bf16[32,1024,8,64]{1,3,2,0:T(8,128)(2,1)} %param.5, f32[32,8,8,1024]{3,2,1,0:T(8,128)S(1)} %copy-done.3, f32[32,8,8]{2,1,0:T(8,128)S(1)} %get-tuple-element.7), kind=kOutput, calls=%fused_computation.10 | convolution fusion | flops 274726912 | bytes 42475520 | tf_op jit(solution)/shard_map/bgsu,bugd->bgsd/dot_general | solution.py:8
  43.8 1.6 copy.25
  45.4 2.6 %copy.26 = f32[32,8,8,1]{3,2,1,0:T(8,128)} copy(f32[32,8,8,1]{2,1,0,3:T(8,128)S(1)} %bitcast.21) | data formatting | bytes 16384 | tf_op jit(solution)/shard_map/broadcast_in_dim | solution.py:14
  47.9 2.9 %pad_maximum_fusion = f32[32,8,8,66]{3,2,1,0:T(8,128)} fusion(f32[32,8,8,1]{3,2,1,0:T(8,128)} %copy.26, f32[32,8,8,1]{3,2,1,0:T(8,128)S(1)} %copy.25, f32[32,8,8,64]{3,2,1,0:T(8,128)S(1)} %fusion.4), kind=kLoop, calls=%fused_computation.13 | loop fusion | flops 270336 | bytes 1081344 | tf_op jit(solution)/shard_map/concatenate | solution.py:17
  50.8 0.1 all-gather.3.cloned.1.call-update
  50.9 95.2 %all-gather.3.cloned.1.call-done = f32[256,8,8,66]{3,2,1,0:T(8,128)} async-done(((f32[32,8,8,66]{3,2,1,0:T(8,128)}), f32[256,8,8,66]{3,2,1,0:T(8,128)}) %all-gather.3.cloned.1.call-update) | async-done | bytes 4325392 | tf_op jit(solution)/shard_map/all_gather | solution.py:28
  146.1 0.0 copy-start.2
  146.1 6.1 %slice_reduce_fusion = f32[32,8,8]{2,1,0:T(8,128)S(1)} fusion(f32[8,32,8,8,66]{4,3,2,1,0:T(8,128)} %bitcast.17), kind=kLoop, calls=%fused_computation.6 | loop fusion | flops 14336 | bytes 73728 | tf_op jit(solution)/shard_map/reduce_max | solution.py:22
  152.2 0.0 copy-done.2
  152.2 7.1 %fusion = (f32[32,8,8]{2,1,0:T(8,128)S(1)}, f32[8,32,8,8,1]{4,3,2,1,0:T(8,128)}) fusion(f32[8,32,8,8,66]{4,3,2,1,0:T(8,128)S(1)} %bitcast.19, f32[32,8,8]{2,1,0:T(8,128)S(1)} %slice_reduce_fusion), kind=kLoop, calls=%fused_computation.1 | loop fusion | flops 47104 | bytes 212992 | tf_op jit(solution)/shard_map/reduce_sum | solution.py:23
  159.3 0.1 copy.29
  159.4 0.1 copy.30
  159.5 0.0 copy-start.1
  159.5 13.8 %copy.35 = f32[8,32,8,8,1]{3,2,1,0,4:T(8,128)S(1)} copy(f32[8,32,8,8,1]{4,3,2,1,0:T(8,128)} %get-tuple-element.6) | data formatting | bytes 131072 | tf_op jit(solution)/shard_map/mul | solution.py:23
  173.3 5.3 %fusion.1 = f32[32,8,8,64]{3,2,1,0:T(8,128)S(1)} fusion(f32[8,32,8,8,66]{4,3,2,1,0:T(8,128)} %bitcast.18, f32[8,32,8,8]{3,2,1,0:T(8,128)S(1)} %bitcast.20), kind=kLoop, calls=%fused_computation.3 | loop fusion | flops 1966080 | bytes 4784128 | tf_op jit(solution)/shard_map/reduce_sum | solution.py:23
  178.6 1.1 fusion.8
  179.8 0.0 copy-done.1
Async XLA Ops:
  6.5 1.0 copy-start
  6.6 139.6 %all-gather.3.cloned.1.call-start = ((), (), s32[]{:S(2)}) async-start(), calls=%async_computation | async-start | bytes 9437184 | tf_op jit(solution)/shard_map/all_gather | solution.py:28
  23.9 5.8 %copy-start.3 = (f32[32,8,8,1024]{3,2,1,0:T(8,128)S(1)}, f32[32,8,8,1024]{3,2,1,0:T(8,128)}, u32[]{:S(2)}) copy-start(f32[32,8,8,1024]{3,2,1,0:T(8,128)} %get-tuple-element.8) | copy-start | bytes 25165828
  146.1 6.1 %copy-start.2 = (f32[256,8,8,66]{3,2,1,0:T(8,128)S(1)}, f32[256,8,8,66]{3,2,1,0:T(8,128)}, u32[]{:S(2)}) copy-start(f32[256,8,8,66]{3,2,1,0:T(8,128)} %all-gather.3.cloned.1.call-done) | copy-start | bytes 12976132
  159.5 20.3 %copy-start.1 = (bf16[32,64,64]{2,1,0:T(8,128)(2,1)S(1)}, bf16[32,64,64]{2,1,0:T(8,128)(2,1)}, u32[]{:S(2)}) copy-start(bf16[32,64,64]{2,1,0:T(8,128)(2,1)} %param.3) | copy-start | bytes 786436
Sparse Core Ops, SparseCore 0:
  51.0 95.0 all-gather.2
where the time goes:
time: 187 us
  waiting for transfers between devices  95.3 us (51%)
  matrix products  30.4 us (16%)
  other arithmetic  27.2 us (15%)
  local copies, waits for them, and re-layouts  20.3 us (11%)
  between operations  13.5 us (7%)
    all_gather x1, waiting for transfers between devices, step(): return together(lax.all_gather(part_of(q, k, v), 'sp')).reshape(q.shape)  95.2 us
    dot_general x2, matrix products, einsum(): return jnp.einsum(form, a.astype(jnp.float32), b.astype(jnp.float32))  30.4 us
    mul x1, local copies, waits for them, and re-layouts, together(): seen * scale  13.8 us
    reduce_sum x1, other arithmetic, together(): jnp.sum(total * scale, 0)  7.07 us
    reduce_max x1, other arithmetic, together(): scale = jnp.exp(high - jnp.max(high, 0))  6.06 us
    reduce_sum x1, other arithmetic, together(): jnp.sum(seen * scale, 0) / jnp.sum(total * scale, 0)  5.31 us
    reduce_sum x1, other arithmetic, part_of(): jnp.sum(weights, -1, keepdims=True)  4.7 us
  transfers between devices with their start and end apart: 1, of which 1 were waited for; matrix products, arithmetic and copies ran while one was open for 0% of the time, Pallas kernels for 0%

commit v1 on v0

v1 whole, which is shorter than its diff:
```python
import functools
import math

import jax
import jax.numpy as jnp
from jax import lax
from jax.experimental import pallas as pl
from jax.experimental.pallas import tpu as pltpu
from jax.sharding import PartitionSpec as P

MESH = pl.DeviceIdType.MESH
F32, BF16 = jnp.float32, jnp.bfloat16
SLOTS = 8
LAG = 2


def kernel(n, q_ref, k_ref, v_ref, out_ref, kbuf, vbuf, qq, pbuf, stage, stat, part, parts, stats, result, ksem, vsem, part_send, part_recv, stat_send, stat_recv, res_send, res_recv):
    batch, heads, head = q_ref.shape
    tokens = k_ref.shape[2]
    kv_heads = k_ref.shape[1] // head
    share = heads // kv_heads
    half = kv_heads // 2
    rows = half * share
    wide = half * head
    pairs = batch // 2
    chunks = pairs // 2
    sub = head // n
    scale = head**-0.5 * math.log2(math.e)
    me = lax.axis_index("sp")
    order = [n // 2] + [s for t in range(n // 2 - 1, 0, -1) for s in (t, n - t)]
    peers = [lax.rem(me + t, n) for t in order]

    def fetch(hbm, buf, sem, b):
        slot = lax.rem(b, SLOTS)
        return pltpu.make_async_copy(hbm.at[b], buf.at[slot], sem.at[slot])

    for b in range(SLOTS):
        fetch(k_ref, kbuf, ksem, b).start()
        fetch(v_ref, vbuf, vsem, b).start()

    barrier = pltpu.get_barrier_semaphore()
    for peer in peers:
        pl.semaphore_signal(barrier, inc=1, device_id={"sp": peer}, device_id_type=MESH)

    q = q_ref[...]
    qq[...] = jnp.concatenate([q, q], -1)

    def of(x, c):
        return x.at[c, pl.ds(0, n - 1)]

    def scores(i):
        own = (lax.broadcasted_iota(jnp.int32, (rows, wide), 0) // share) == (lax.broadcasted_iota(jnp.int32, (rows, wide), 1) // head)
        highs, sums = [], []
        for t in range(2):
            b = 2 * i + t
            slot = lax.rem(b, SLOTS)
            fetch(k_ref, kbuf, ksem, b).wait()
            for h in range(2):
                x = qq[b, pl.ds(h * rows, rows), :]
                x = jnp.where(own, jnp.concatenate([x] * (wide // (2 * head)), -1), jnp.zeros((), BF16))
                s = jnp.dot(x, kbuf[slot, pl.ds(h * wide, wide), :], preferred_element_type=F32)
                high = jnp.max(s, -1, keepdims=True)
                w = jnp.exp2((s - high) * scale)
                pbuf[lax.rem(i, 2), t, pl.ds(h * rows, rows), :] = w.astype(BF16)
                highs.append(high)
                sums.append(jnp.sum(w, -1, keepdims=True))
        high, total = jnp.concatenate(highs, 0), jnp.concatenate(sums, 0)
        lane = lax.broadcasted_iota(jnp.int32, (2 * heads, 128), 1)
        stat[i // 2, pl.ds(2 * lax.rem(i, 2), 2), :] = jnp.where(lane == 0, high, total).T[:2]

    def values(i):
        seen = []
        for t in range(2):
            b = 2 * i + t
            slot = lax.rem(b, SLOTS)
            fetch(v_ref, vbuf, vsem, b).wait()
            r = lax.dot_general(vbuf[slot], pbuf[lax.rem(i, 2), t], (((1,), (1,)), ((), ())), preferred_element_type=F32)
            lane = lax.broadcasted_iota(jnp.int32, (head, heads), 1) // share
            o = r[:head]
            for g in range(1, kv_heads):
                o = jnp.where(lane == g, r[g * head : (g + 1) * head], o)
            seen.append(o)
        stage[:, pl.ds(lax.rem(i, 2), 1)] = jnp.concatenate(seen, 1).reshape(n, 1, sub, 2 * heads)

    def send(c):
        part[c] = stage[...].reshape(n, 2 * sub, 2 * heads).astype(BF16)
        parts[c, me] = part[c, me]
        stats[c, me] = stat[c]
        for peer in peers:
            pltpu.make_async_remote_copy(stat.at[c], stats.at[c, me], stat_send.at[c], stat_recv.at[c], device_id={"sp": peer}, device_id_type=MESH).start()
            pltpu.make_async_remote_copy(part.at[c, peer], parts.at[c, me], part_send.at[c], part_recv.at[c], device_id={"sp": peer}, device_id_type=MESH).start()

    def wait_recv(x, c, send_sem, recv_sem):
        pltpu.make_async_remote_copy(of(x, c), of(x, c), send_sem.at[c], recv_sem.at[c], device_id={"sp": peers[0]}, device_id_type=MESH).wait_recv()

    def wait_send(x, c, send_sem, recv_sem):
        pltpu.make_async_remote_copy(of(x, c), of(x, c), send_sem.at[c], recv_sem.at[c], device_id={"sp": peers[0]}, device_id_type=MESH).wait_send()

    def combine(c):
        wait_recv(stats, c, stat_send, stat_recv)
        wait_recv(parts, c, part_send, part_recv)
        highs = [stats[c, d, pl.ds(0, 4), :] for d in range(n)]
        top = functools.reduce(jnp.maximum, highs)
        top_of = [jnp.broadcast_to(top[2 * p : 2 * p + 1], (sub, 2 * heads)) for p in range(2)]
        acc, total = [0.0, 0.0], [0.0, 0.0]
        for d in range(n):
            x = parts[c, d].astype(F32)
            for p in range(2):
                e = jnp.exp2((highs[d][2 * p : 2 * p + 1] - top_of[p]) * scale)
                acc[p] += x[p * sub : (p + 1) * sub] * e
                total[p] += highs[d][2 * p + 1 : 2 * p + 2] * e
        result[c, me] = jnp.concatenate([acc[p] / total[p] for p in range(2)], 0).astype(BF16)
        for peer in peers:
            pltpu.make_async_remote_copy(result.at[c, me], result.at[c, me], res_send.at[c], res_recv.at[c], device_id={"sp": peer}, device_id_type=MESH).start()

    def finish(c):
        wait_recv(result, c, res_send, res_recv)
        x = result[c].astype(F32)
        for p in range(2):
            y = x[:, p * sub : (p + 1) * sub].reshape(head, 2 * heads).T.astype(BF16)
            out_ref[pl.ds(4 * c + 2 * p, 2)] = y.reshape(2, heads, head)

    def refill(hbm, buf, sem, i):
        @pl.when(2 * i < batch)
        def _():
            for t in range(2):
                fetch(hbm, buf, sem, 2 * i + t).start()

    scores(0)
    refill(k_ref, kbuf, ksem, SLOTS // 2)
    pl.semaphore_wait(barrier, n - 1)

    def after(i):
        c = i // 2

        @pl.when(lax.rem(i, 2) == 1)
        def _():
            send(c)

            @pl.when(c >= LAG)
            def _():
                combine(c - LAG)

            @pl.when(c >= 2 * LAG)
            def _():
                finish(c - 2 * LAG)

    def step(i, carry):
        scores(i + 1)
        values(i)
        refill(k_ref, kbuf, ksem, i + 1 + SLOTS // 2)
        refill(v_ref, vbuf, vsem, i + SLOTS // 2)
        after(i)
        return carry

    lax.fori_loop(0, pairs - 1, step, 0)
    values(pairs - 1)
    after(jnp.int32(pairs - 1))
    for c in range(chunks - LAG, chunks):
        combine(c)
    for c in range(max(chunks - 2 * LAG, 0), chunks):
        finish(c)
    for c in range(chunks):
        wait_send(parts, c, part_send, part_recv)
        wait_send(stats, c, stat_send, stat_recv)
        wait_send(result, c, res_send, res_recv)


def solution(mesh):
    n = mesh.shape["sp"]

    def step(q, k, v):
        batch, heads, head = q.shape
        _, tokens, kv_heads, _ = k.shape
        k = k.transpose(0, 2, 3, 1).reshape(batch, kv_heads * head, tokens)
        v = v.transpose(0, 2, 3, 1).reshape(batch, kv_heads * head, tokens)
        chunks, sub = batch // 4, head // n
        dma = pltpu.SemaphoreType.DMA
        return pl.pallas_call(
            functools.partial(kernel, n),
            out_shape=jax.ShapeDtypeStruct(q.shape, BF16),
            in_specs=[pl.BlockSpec(memory_space=pltpu.VMEM), pl.BlockSpec(memory_space=pl.ANY), pl.BlockSpec(memory_space=pl.ANY)],
            out_specs=pl.BlockSpec(memory_space=pltpu.VMEM),
            scratch_shapes=[
                pltpu.VMEM((SLOTS, kv_heads * head, tokens), BF16),
                pltpu.VMEM((SLOTS, kv_heads * head, tokens), BF16),
                pltpu.VMEM((batch, heads, 2 * head), BF16),
                pltpu.VMEM((2, 2, heads, tokens), BF16),
                pltpu.VMEM((n, 2, sub, 2 * heads), F32),
                pltpu.VMEM((chunks, 8, 2 * heads), F32),
                pltpu.VMEM((chunks, n, 2 * sub, 2 * heads), BF16),
                pltpu.VMEM((chunks, n, 2 * sub, 2 * heads), BF16),
                pltpu.VMEM((chunks, n, 8, 2 * heads), F32),
                pltpu.VMEM((chunks, n, 2 * sub, 2 * heads), BF16),
                dma((SLOTS,)),
                dma((SLOTS,)),
            ]
            + [dma((chunks,))] * 6,
            compiler_params=pltpu.CompilerParams(collective_id=0, has_side_effects=True, vmem_limit_bytes=60 * 2**20),
        )(q, k, v)

    return jax.shard_map(
        step,
        mesh=mesh,
        in_specs=(P("dp", None, None), P("dp", "sp", None, None), P("dp", "sp", None, None)),
        out_specs=P("dp", None, None),
        check_vma=False,
    )
```

time: 187 us -> 65.1 us (0.35)
  the two profiles are of different devices: /device:TPU:21 before, /device:TPU:22 now
where the time goes in v1:
time: 65.1 us; the launch traced here: 65 us
  Pallas kernels  63.1 us (97%)
  local copies, waits for them, and re-layouts  1.87 us (3%)
    pallas_call x1, Pallas kernels, step(): pl.pallas_call(functools.partial(kernel, n), out_shape=jax.ShapeDtypeStru...  63.1 us
    unnamed x1, local copies, waits for them, and re-layouts  1.87 us

profile of v1, /device:TPU:22, one launch (start us, length us, event | category | flops | bytes accessed | tf_op | source)
XLA Modules:
  0.0 65.0 jit_solution(11310073995187700725)
XLA Ops:
  0.0 63.1 %shard_map.37 = bf16[32,64,64]{2,1,0:T(8,128)(2,1)} custom-call(bf16[32,64,64]{2,1,0:T(8,128)(2,1)} %q_ref.1, bf16[32,512,1024]{2,1,0:T(8,128)(2,1)} %bitcast.6, bf16[32,512,1024]{2,1,0:T(8,128)(2,1)} %bitcast.7), custom_call_target="tpu_custom_call" | custom-call | tf_op jit(solution)/shard_map/pallas_call | solution.py:179
  63.1 1.9 %copy.5 = bf16[32,64,64]{2,1,0:T(8,128)(2,1)} copy(bf16[32,64,64]{2,1,0:T(8,128)(2,1)} %shard_map.37) | data formatting | bytes 524288

commit v2 on v1

v2 whole, which is shorter than its diff:
```python
import functools
import math

import jax
import jax.numpy as jnp
from jax import lax
from jax.experimental import pallas as pl
from jax.experimental.pallas import tpu as pltpu
from jax.sharding import PartitionSpec as P

MESH = pl.DeviceIdType.MESH
F32, BF16 = jnp.float32, jnp.bfloat16
TILE = 256
SLOTS = 8
LAG = 3


def kernel(n, q_ref, k_ref, v_ref, out_ref, qbuf, kbuf, vbuf, qq, sbuf, pbuf, stage, stat, part, parts, stats, result, qsem, ksem, vsem, part_send, part_recv, stat_send, stat_recv, res_send, res_recv):
    batch, heads, head = q_ref.shape
    tokens = k_ref.shape[2]
    kv_heads = k_ref.shape[1] // head
    share = heads // kv_heads
    half = kv_heads // 2
    rows = half * share
    wide = half * head
    pairs = batch // 2
    chunks = pairs // 2
    sub = head // n
    scale = head**-0.5 * math.log2(math.e)
    me = lax.axis_index("sp")
    order = [n // 2] + [s for t in range(n // 2 - 1, 0, -1) for s in (t, n - t)]
    peers = [lax.rem(me + t, n) for t in order]

    def fetch(hbm, buf, sem, b):
        slot = lax.rem(b, SLOTS)
        return pltpu.make_async_copy(hbm.at[b], buf.at[slot], sem.at[slot])

    keys, vals = (k_ref, kbuf, ksem), (v_ref, vbuf, vsem)

    def start(x, i):
        for t in range(2):
            fetch(*x, 2 * i + t).start()

    def wait(x, i):
        for t in range(2):
            fetch(*x, 2 * i + t).wait()

    def refill(x, i):
        @pl.when(i < pairs)
        def _():
            start(x, i)

    ahead = SLOTS // 2


    start(keys, 0)
    start(keys, 1)
    start(vals, 0)
    start(keys, 2)
    start(vals, 1)

    barrier = pltpu.get_barrier_semaphore()
    for peer in peers:
        pl.semaphore_signal(barrier, inc=1, device_id={"sp": peer}, device_id_type=MESH)


    q = q_ref[...]
    qq[...] = jnp.concatenate([q, q], -1)

    def of(x, c):
        return x.at[c, pl.ds(0, n - 1)]

    def query(i):
        own = (lax.broadcasted_iota(jnp.int32, (rows, wide), 0) // share) == (lax.broadcasted_iota(jnp.int32, (rows, wide), 1) // head)
        x = []
        for t in range(2):
            for h in range(2):
                y = qq[2 * i + t, pl.ds(h * rows, rows), :]
                x.append(jnp.where(own, jnp.concatenate([y] * (wide // (2 * head)), -1), jnp.zeros((), BF16)))
        return x

    def weigh(i, side):
        highs, sums = [], []
        for t in range(2):
            for h in range(2):
                x = sbuf[side, t, pl.ds(h * rows, rows), :]
                high = jnp.max(x, -1, keepdims=True)
                w = jnp.exp2((x - high) * scale)
                pbuf[side, t, pl.ds(h * rows, rows), :] = w.astype(BF16)
                highs.append(high)
                sums.append(jnp.sum(w, -1, keepdims=True))
        high, total = jnp.concatenate(highs, 0), jnp.concatenate(sums, 0)
        lane = lax.broadcasted_iota(jnp.int32, (2 * heads, 128), 1)
        stat[i // 2, pl.ds(2 * side, 2), :] = jnp.where(lane == 0, high, total).T[:2]

    steps = tokens // TILE

    def block(i, side, scores, weights, values):
        if weights:
            weigh(i + 1, 1 - side)
        if scores:
            x = query(i + 2)
        seen = [[None, None], [None, None]]
        for h in range(2):
            for c in range(steps):
                for t in range(2):
                    if values:
                        a = vbuf[lax.rem(2 * i + t, SLOTS), pl.ds(h * wide, wide), pl.ds(c * TILE, TILE)]
                        p = pbuf[side, t, pl.ds(h * rows, rows), pl.ds(c * TILE, TILE)]
                        d = lax.dot_general(a, p, (((1,), (1,)), ((), ())), preferred_element_type=F32)
                        seen[t][h] = d if c == 0 else seen[t][h] + d
                    if scores:
                        y = kbuf[lax.rem(2 * i + 4 + t, SLOTS), pl.ds(h * wide, wide), pl.ds(c * TILE, TILE)]
                        sbuf[side, t, pl.ds(h * rows, rows), pl.ds(c * TILE, TILE)] = jnp.dot(x[2 * t + h], y, preferred_element_type=F32)
        if values:
            lane = lax.broadcasted_iota(jnp.int32, (head, rows), 1) // share
            own = []
            for t in range(2):
                for h in range(2):
                    o = seen[t][h][:head]
                    for g in range(1, half):
                        o = jnp.where(lane == g, seen[t][h][g * head : (g + 1) * head], o)
                    own.append(o)
            stage[:, side] = jnp.concatenate(own, 1).reshape(n, sub, 2 * heads)

    def send(c):
        part[c] = stage[...].reshape(n, 2 * sub, 2 * heads).astype(BF16)
        parts[c, me] = part[c, me]
        stats[c, me] = stat[c]
        for peer in peers:
            pltpu.make_async_remote_copy(stat.at[c], stats.at[c, me], stat_send.at[c], stat_recv.at[c], device_id={"sp": peer}, device_id_type=MESH).start()
            pltpu.make_async_remote_copy(part.at[c, peer], parts.at[c, me], part_send.at[c], part_recv.at[c], device_id={"sp": peer}, device_id_type=MESH).start()

    def wait_recv(x, c, send_sem, recv_sem):
        pltpu.make_async_remote_copy(of(x, c), of(x, c), send_sem.at[c], recv_sem.at[c], device_id={"sp": peers[0]}, device_id_type=MESH).wait_recv()

    def wait_send(x, c, send_sem, recv_sem):
        pltpu.make_async_remote_copy(of(x, c), of(x, c), send_sem.at[c], recv_sem.at[c], device_id={"sp": peers[0]}, device_id_type=MESH).wait_send()

    def combine(c):
        wait_recv(stats, c, stat_send, stat_recv)
        wait_recv(parts, c, part_send, part_recv)
        highs = [stats[c, d] for d in range(n)]
        top = functools.reduce(jnp.maximum, highs)
        top_of = [jnp.broadcast_to(top[2 * p : 2 * p + 1], (sub, 2 * heads)) for p in range(2)]
        acc, total = [0.0, 0.0], [0.0, 0.0]
        for d in range(n):
            x = parts[c, d].astype(F32)
            for p in range(2):
                e = jnp.exp2((highs[d][2 * p : 2 * p + 1] - top_of[p]) * scale)
                acc[p] += x[p * sub : (p + 1) * sub] * e
                total[p] += highs[d][2 * p + 1 : 2 * p + 2] * e
        result[c, me] = jnp.concatenate([acc[p] / total[p] for p in range(2)], 0).astype(BF16)
        for peer in peers:
            pltpu.make_async_remote_copy(result.at[c, me], result.at[c, me], res_send.at[c], res_recv.at[c], device_id={"sp": peer}, device_id_type=MESH).start()

    def finish(c):
        wait_recv(result, c, res_send, res_recv)
        x = result[c].astype(F32)
        for p in range(2):
            y = x[:, p * sub : (p + 1) * sub].reshape(head, 2 * heads).T.astype(BF16)
            out_ref[pl.ds(4 * c + 2 * p, 2)] = y.reshape(2, heads, head)

    wait(keys, 0)
    block(-2, 0, True, False, False)
    start(keys, 3)
    start(vals, 2)
    wait(keys, 1)
    block(-1, 1, True, True, False)
    start(keys, 4)
    start(vals, 3)
    start(keys, 5)
    pl.semaphore_wait(barrier, n - 1)

    def step(c, carry):
        for side in range(2):
            i = 2 * c + side
            wait(keys, i + 2)
            wait(vals, i)
            block(i, side, True, True, True)
            refill(keys, i + 2 + ahead)
            refill(vals, i + ahead)
        send(c)

        @pl.when(c >= LAG)
        def _():
            combine(c - LAG)

        @pl.when(c >= 2 * LAG)
        def _():
            finish(c - 2 * LAG)

        return carry

    last = chunks - 1
    lax.fori_loop(0, last, step, 0)
    wait(vals, pairs - 2)
    block(pairs - 2, 0, False, True, True)
    wait(vals, pairs - 1)
    block(pairs - 1, 1, False, False, True)
    send(last)
    for c in range(last - LAG, chunks):
        combine(c)
    for c in range(max(last - 2 * LAG, 0), chunks):
        finish(c)
    for c in range(chunks):
        wait_send(parts, c, part_send, part_recv)
        wait_send(stats, c, stat_send, stat_recv)
        wait_send(result, c, res_send, res_recv)


def solution(mesh):
    n = mesh.shape["sp"]

    def step(q, k, v):
        batch, heads, head = q.shape
        _, tokens, kv_heads, _ = k.shape
        k = k.transpose(0, 2, 3, 1).reshape(batch, kv_heads * head, tokens)
        v = v.transpose(0, 2, 3, 1).reshape(batch, kv_heads * head, tokens)
        chunks, sub = batch // 4, head // n
        dma = pltpu.SemaphoreType.DMA
        return pl.pallas_call(
            functools.partial(kernel, n),
            out_shape=jax.ShapeDtypeStruct(q.shape, BF16),
            in_specs=[pl.BlockSpec(memory_space=pltpu.VMEM), pl.BlockSpec(memory_space=pl.ANY), pl.BlockSpec(memory_space=pl.ANY)],
            out_specs=pl.BlockSpec(memory_space=pltpu.VMEM),
            scratch_shapes=[
                pltpu.VMEM(q.shape, BF16),
                pltpu.VMEM((SLOTS, kv_heads * head, tokens), BF16),
                pltpu.VMEM((SLOTS, kv_heads * head, tokens), BF16),
                pltpu.VMEM((batch, heads, 2 * head), BF16),
                pltpu.VMEM((2, 2, heads, tokens), F32),
                pltpu.VMEM((2, 2, heads, tokens), BF16),
                pltpu.VMEM((n, 2, sub, 2 * heads), F32),
                pltpu.VMEM((chunks, 4, 2 * heads), F32),
                pltpu.VMEM((chunks, n, 2 * sub, 2 * heads), BF16),
                pltpu.VMEM((chunks, n, 2 * sub, 2 * heads), BF16),
                pltpu.VMEM((chunks, n, 4, 2 * heads), F32),
                pltpu.VMEM((chunks, n, 2 * sub, 2 * heads), BF16),
                dma,
                dma((SLOTS,)),
                dma((SLOTS,)),
            ]
            + [dma((chunks,))] * 6,
            compiler_params=pltpu.CompilerParams(collective_id=0, has_side_effects=True, vmem_limit_bytes=28 * 2**20),
        )(q, k, v)

    return jax.shard_map(
        step,
        mesh=mesh,
        in_specs=(P("dp", None, None), P("dp", "sp", None, None), P("dp", "sp", None, None)),
        out_specs=P("dp", None, None),
        check_vma=False,
    )
```

time: 65.1 us -> 39.2 us (0.60)
  Pallas kernels: 63.1 us -> 37.3 us
    pallas_call x1, Pallas kernels: 63.1 us -> 37.3 us  [step(): pl.pallas_call(functools.partial(kernel, n), out_shape=jax.ShapeDtypeStru...]
    unnamed x1 -> x3, local copies, waits for them, and re-layouts: 1.87 us -> 1.84 us
where the time goes in v2:
time: 39.2 us; the launch traced here: 39.1 us
  Pallas kernels  37.3 us (95%)
  local copies, waits for them, and re-layouts  1.84 us (5%)
    pallas_call x1, Pallas kernels, step(): pl.pallas_call(functools.partial(kernel, n), out_shape=jax.ShapeDtypeStru...  37.3 us
    unnamed x3, local copies, waits for them, and re-layouts  1.84 us

profile of v2, /device:TPU:22, one launch (start us, length us, event | category | flops | bytes accessed | tf_op | source)
XLA Modules:
  0.0 39.1 jit_solution(12081041401194748671)
XLA Ops:
  0.0 0.0 copy-start
  0.0 1.0 %copy-done = bf16[32,64,64]{2,1,0:T(8,128)(2,1)S(1)} copy-done((bf16[32,64,64]{2,1,0:T(8,128)(2,1)S(1)}, bf16[32,64,64]{2,1,0:T(8,128)(2,1)}, u32[]{:S(2)}) %copy-start) | copy-done | bytes 262168
  1.0 37.3 %shard_map.37 = bf16[32,64,64]{2,1,0:T(8,128)(2,1)S(1)} custom-call(bf16[32,64,64]{2,1,0:T(8,128)(2,1)S(1)} %copy-done, bf16[32,512,1024]{2,1,0:T(8,128)(2,1)} %bitcast.6, bf16[32,512,1024]{2,1,0:T(8,128)(2,1)} %bitcast.7), custom_call_target="tpu_custom_call" | custom-call | tf_op jit(solution)/shard_map/pallas_call | solution.py:222
  38.3 0.8 %copy.5 = bf16[32,64,64]{2,1,0:T(8,128)(2,1)} copy(bf16[32,64,64]{2,1,0:T(8,128)(2,1)S(1)} %shard_map.37) | data formatting | bytes 524288
Async XLA Ops:
  0.0 1.0 %copy-start = (bf16[32,64,64]{2,1,0:T(8,128)(2,1)S(1)}, bf16[32,64,64]{2,1,0:T(8,128)(2,1)}, u32[]{:S(2)}) copy-start(bf16[32,64,64]{2,1,0:T(8,128)(2,1)} %q_ref.1) | copy-start | bytes 786436

commit v3 on v2

--- a/solution.py
+++ b/solution.py
@@ -13,9 +13,10 @@
 TILE = 256
 SLOTS = 8
 LAG = 3
-
-
-def kernel(n, q_ref, k_ref, v_ref, out_ref, qbuf, kbuf, vbuf, qq, sbuf, pbuf, stage, stat, part, parts, stats, result, qsem, ksem, vsem, part_send, part_recv, stat_send, stat_recv, res_send, res_recv):
+LATE = 2
+
+
+def kernel(n, q_ref, k_ref, v_ref, out_ref, qbuf, kbuf, vbuf, qq, sbuf, pbuf, stage, stat, part, parts, stats, result, late_stat, late_stats, late, lates, late_result, qsem, ksem, vsem, part_send, part_recv, stat_send, stat_recv, res_send, res_recv, late_stat_send, late_stat_recv, late_send, late_recv, late_res_send, late_res_recv):
     batch, heads, head = q_ref.shape
     tokens = k_ref.shape[2]
     kv_heads = k_ref.shape[1] // head
@@ -24,7 +25,8 @@
     rows = half * share
     wide = half * head
     pairs = batch // 2
-    chunks = pairs // 2
+    chunks = (pairs - LATE) // 2
+    owners = n // 2
     sub = head // n
     scale = head**-0.5 * math.log2(math.e)
     me = lax.axis_index("sp")
@@ -45,26 +47,32 @@
         for t in range(2):
             fetch(*x, 2 * i + t).wait()
 
-    def refill(x, i):
-        @pl.when(i < pairs)
-        def _():
-            start(x, i)
-
     ahead = SLOTS // 2
 
-
+    def more(i):
+        @pl.when(i + 2 + ahead < pairs)
+        def _():
+            start(keys, i + 2 + ahead)
+
+        @pl.when(i + ahead < pairs)
+        def _():
+            start(vals, i + ahead)
+
+    load_q = pltpu.make_async_copy(q_ref, qbuf, qsem)
+    load_q.start()
     start(keys, 0)
     start(keys, 1)
     start(vals, 0)
-    start(keys, 2)
-    start(vals, 1)
+    for p in range(2, ahead):
+        start(keys, p)
+        start(vals, p - 1)
 
     barrier = pltpu.get_barrier_semaphore()
     for peer in peers:
         pl.semaphore_signal(barrier, inc=1, device_id={"sp": peer}, device_id_type=MESH)
 
-
-    q = q_ref[...]
+    load_q.wait()
+    q = qbuf[...]
     qq[...] = jnp.concatenate([q, q], -1)
 
     def of(x, c):
@@ -123,53 +131,113 @@
                     own.append(o)
             stage[:, side] = jnp.concatenate(own, 1).reshape(n, sub, 2 * heads)
 
+    def push(src, dst, send_sem, recv_sem, peer):
+        pltpu.make_async_remote_copy(src, dst, send_sem, recv_sem, device_id={"sp": peer}, device_id_type=MESH).start()
+
+    def arrive(x, recv_sem):
+        pltpu.make_async_remote_copy(x, x, recv_sem, recv_sem, device_id={"sp": peers[0]}, device_id_type=MESH).wait_recv()
+
+    def left(x, send_sem):
+        pltpu.make_async_remote_copy(x, x, send_sem, send_sem, device_id={"sp": peers[0]}, device_id_type=MESH).wait_send()
+
+    def weights_of(rows_of, p, size):
+        top = functools.reduce(jnp.maximum, [x[2 * p : 2 * p + 1] for x in rows_of])
+        e = [jnp.exp2((x[2 * p : 2 * p + 1] - top) * scale) for x in rows_of]
+        total = functools.reduce(jnp.add, [x[2 * p + 1 : 2 * p + 2] * y for x, y in zip(rows_of, e)])
+        shape = (size, 2 * heads)
+        return [jnp.broadcast_to(y, shape) for y in e], jnp.broadcast_to(total, shape)
+
+    def show(b, x):
+        out_ref[pl.ds(b, 2)] = x.T.astype(BF16).reshape(2, heads, head)
+
     def send(c):
         part[c] = stage[...].reshape(n, 2 * sub, 2 * heads).astype(BF16)
         parts[c, me] = part[c, me]
         stats[c, me] = stat[c]
         for peer in peers:
-            pltpu.make_async_remote_copy(stat.at[c], stats.at[c, me], stat_send.at[c], stat_recv.at[c], device_id={"sp": peer}, device_id_type=MESH).start()
-            pltpu.make_async_remote_copy(part.at[c, peer], parts.at[c, me], part_send.at[c], part_recv.at[c], device_id={"sp": peer}, device_id_type=MESH).start()
-
-    def wait_recv(x, c, send_sem, recv_sem):
-        pltpu.make_async_remote_copy(of(x, c), of(x, c), send_sem.at[c], recv_sem.at[c], device_id={"sp": peers[0]}, device_id_type=MESH).wait_recv()
-
-    def wait_send(x, c, send_sem, recv_sem):
-        pltpu.make_async_remote_copy(of(x, c), of(x, c), send_sem.at[c], recv_sem.at[c], device_id={"sp": peers[0]}, device_id_type=MESH).wait_send()
+            push(stat.at[c], stats.at[c, me], stat_send.at[c], stat_recv.at[c], peer)
+            push(part.at[c, peer], parts.at[c, me], part_send.at[c], part_recv.at[c], peer)
 
     def combine(c):
-        wait_recv(stats, c, stat_send, stat_recv)
-        wait_recv(parts, c, part_send, part_recv)
-        highs = [stats[c, d] for d in range(n)]
-        top = functools.reduce(jnp.maximum, highs)
-        top_of = [jnp.broadcast_to(top[2 * p : 2 * p + 1], (sub, 2 * heads)) for p in range(2)]
-        acc, total = [0.0, 0.0], [0.0, 0.0]
-        for d in range(n):
-            x = parts[c, d].astype(F32)
-            for p in range(2):
-                e = jnp.exp2((highs[d][2 * p : 2 * p + 1] - top_of[p]) * scale)
-                acc[p] += x[p * sub : (p + 1) * sub] * e
-                total[p] += highs[d][2 * p + 1 : 2 * p + 2] * e
-        result[c, me] = jnp.concatenate([acc[p] / total[p] for p in range(2)], 0).astype(BF16)
+        arrive(of(stats, c), stat_recv.at[c])
+        arrive(of(parts, c), part_recv.at[c])
+        seen = [stats[c, d] for d in range(n)]
+        both = []
+        x = [parts[c, d].astype(F32) for d in range(n)]
+        for p in range(2):
+            e, total = weights_of(seen, p, sub)
+            both.append(functools.reduce(jnp.add, [x[d][p * sub : (p + 1) * sub] * e[d] for d in range(n)]) / total)
+        result[c, me] = jnp.concatenate(both, 0).astype(BF16)
         for peer in peers:
-            pltpu.make_async_remote_copy(result.at[c, me], result.at[c, me], res_send.at[c], res_recv.at[c], device_id={"sp": peer}, device_id_type=MESH).start()
+            push(result.at[c, me], result.at[c, me], res_send.at[c], res_recv.at[c], peer)
 
     def finish(c):
-        wait_recv(result, c, res_send, res_recv)
+        arrive(of(result, c), res_recv.at[c])
         x = result[c].astype(F32)
         for p in range(2):
-            y = x[:, p * sub : (p + 1) * sub].reshape(head, 2 * heads).T.astype(BF16)
-            out_ref[pl.ds(4 * c + 2 * p, 2)] = y.reshape(2, heads, head)
+            show(4 * c + 2 * p, x[:, p * sub : (p + 1) * sub].reshape(head, 2 * heads))
+
+    mine = lax.rem(me + owners // 2, n)
+    owner = mine < owners
+    device = [(j + n - owners // 2) % n for j in range(owners)]
+
+    def send_late(e):
+        c, side = (pairs - LATE + e) // 2, e % 2
+        late_stat[e] = stat[c, pl.ds(2 * side, 2), :]
+        late[e] = stage[:, side].reshape(owners, 2 * sub, 2 * heads).astype(BF16)
+        for j in range(owners):
+
+            @pl.when(mine != j)
+            def _():
+                push(late_stat.at[e], late_stats.at[e, me], late_stat_send.at[e], late_stat_recv.at[e], device[j])
+                push(late.at[e, j], lates.at[e, me], late_send.at[e], late_recv.at[e], device[j])
+
+            @pl.when(mine == j)
+            def _():
+                late_stats[e, me] = late_stat[e]
+                lates[e, me] = late[e, j]
+
+    def combine_late(e):
+        @pl.when(owner)
+        def _():
+            arrive(of(late_stats, e), late_stat_recv.at[e])
+            arrive(of(lates, e), late_recv.at[e])
+            w, total = weights_of([late_stats[e, d] for d in range(n)], 0, 2 * sub)
+            late_result[e, mine] = (functools.reduce(jnp.add, [lates[e, d].astype(F32) * w[d] for d in range(n)]) / total).astype(BF16)
+            for t in range(n - 1):
+                peer = t + jnp.where(t >= me, 1, 0)
+                push(late_result.at[e, mine], late_result.at[e, mine], late_res_send.at[e], late_res_recv.at[e], peer)
+
+    def finish_late(e):
+        @pl.when(owner)
+        def _():
+            arrive(late_result.at[e, pl.ds(0, owners - 1)], late_res_recv.at[e])
+
+        @pl.when(jnp.logical_not(owner))
+        def _():
+            arrive(late_result.at[e], late_res_recv.at[e])
+
+        show(batch - 2 * LATE + 2 * e, late_result[e].astype(F32).reshape(head, 2 * heads))
+
+    def leave_late(e):
+        @pl.when(owner)
+        def _():
+            left(late_stats.at[e, pl.ds(0, owners - 1)], late_stat_send.at[e])
+            left(lates.at[e, pl.ds(0, owners - 1)], late_send.at[e])
+            left(of(lates, e), late_res_send.at[e])
+
+        @pl.when(jnp.logical_not(owner))
+        def _():
+            left(late_stats.at[e, pl.ds(0, owners)], late_stat_send.at[e])
+            left(lates.at[e, pl.ds(0, owners)], late_send.at[e])
 
     wait(keys, 0)
     block(-2, 0, True, False, False)
-    start(keys, 3)
-    start(vals, 2)
+    start(keys, ahead)
+    start(vals, ahead - 1)
     wait(keys, 1)
     block(-1, 1, True, True, False)
-    start(keys, 4)
-    start(vals, 3)
-    start(keys, 5)
+    start(keys, ahead + 1)
     pl.semaphore_wait(barrier, n - 1)
 
     def step(c, carry):
@@ -178,35 +246,44 @@
             wait(keys, i + 2)
             wait(vals, i)
             block(i, side, True, True, True)
-            refill(keys, i + 2 + ahead)
-            refill(vals, i + ahead)
+
+            more(i)
+
         send(c)
 
         @pl.when(c >= LAG)
         def _():
             combine(c - LAG)
 
-        @pl.when(c >= 2 * LAG)
-        def _():
-            finish(c - 2 * LAG)
-
         return carry
 
-    last = chunks - 1
-    lax.fori_loop(0, last, step, 0)
-    wait(vals, pairs - 2)
-    block(pairs - 2, 0, False, True, True)
-    wait(vals, pairs - 1)
-    block(pairs - 1, 1, False, False, True)
-    send(last)
-    for c in range(last - LAG, chunks):
-        combine(c)
-    for c in range(max(last - 2 * LAG, 0), chunks):
-        finish(c)
-    for c in range(chunks):
-        wait_send(parts, c, part_send, part_recv)
-        wait_send(stats, c, stat_send, stat_recv)
-        wait_send(result, c, res_send, res_recv)
+    lax.fori_loop(0, chunks, step, 0)
+    i = pairs - LATE
+    wait(vals, i)
+    block(i, 0, False, True, True)
+    send_late(0)
+    wait(vals, i + 1)
+    block(i + 1, 1, False, False, True)
+    send_late(1)
+
+    def repeat(f, first, end):
+        def body(c, carry):
+            f(c)
+            return carry
+
+        lax.fori_loop(first, end, body, 0)
+
+    def leave(c):
+        left(of(parts, c), part_send.at[c])
+        left(of(stats, c), stat_send.at[c])
+        left(of(result, c), res_send.at[c])
+
+    repeat(combine, chunks - 3, chunks)
+    repeat(combine_late, 0, LATE)
+    repeat(finish, 0, chunks)
+    repeat(finish_late, 0, LATE)
+    repeat(leave, 0, chunks)
+    repeat(leave_late, 0, LATE)
 
 
 def solution(mesh):
@@ -217,12 +294,13 @@
         _, tokens, kv_heads, _ = k.shape
         k = k.transpose(0, 2, 3, 1).reshape(batch, kv_heads * head, tokens)
         v = v.transpose(0, 2, 3, 1).reshape(batch, kv_heads * head, tokens)
-        chunks, sub = batch // 4, head // n
+        chunks, sub = batch // 4 - LATE // 2, head // n
+        q = pltpu.with_memory_space_constraint(q, pltpu.HBM)
         dma = pltpu.SemaphoreType.DMA
         return pl.pallas_call(
             functools.partial(kernel, n),
             out_shape=jax.ShapeDtypeStruct(q.shape, BF16),
-            in_specs=[pl.BlockSpec(memory_space=pltpu.VMEM), pl.BlockSpec(memory_space=pl.ANY), pl.BlockSpec(memory_space=pl.ANY)],
+            in_specs=[pl.BlockSpec(memory_space=pltpu.HBM)] * 3,
             out_specs=pl.BlockSpec(memory_space=pltpu.VMEM),
             scratch_shapes=[
                 pltpu.VMEM(q.shape, BF16),
@@ -232,16 +310,22 @@
                 pltpu.VMEM((2, 2, heads, tokens), F32),
                 pltpu.VMEM((2, 2, heads, tokens), BF16),
                 pltpu.VMEM((n, 2, sub, 2 * heads), F32),
-                pltpu.VMEM((chunks, 4, 2 * heads), F32),
+                pltpu.VMEM((batch // 4, 4, 2 * heads), F32),
                 pltpu.VMEM((chunks, n, 2 * sub, 2 * heads), BF16),
                 pltpu.VMEM((chunks, n, 2 * sub, 2 * heads), BF16),
                 pltpu.VMEM((chunks, n, 4, 2 * heads), F32),
                 pltpu.VMEM((chunks, n, 2 * sub, 2 * heads), BF16),
+                pltpu.VMEM((LATE, 2, 2 * heads), F32),
+                pltpu.VMEM((LATE, n, 2, 2 * heads), F32),
+                pltpu.VMEM((LATE, n // 2, 2 * sub, 2 * heads), BF16),
+                pltpu.VMEM((LATE, n, 2 * sub, 2 * heads), BF16),
+                pltpu.VMEM((LATE, n // 2, 2 * sub, 2 * heads), BF16),
                 dma,
                 dma((SLOTS,)),
                 dma((SLOTS,)),
             ]
-            + [dma((chunks,))] * 6,
+            + [dma((chunks,))] * 6
+            + [dma((LATE,))] * 6,
             compiler_params=pltpu.CompilerParams(collective_id=0, has_side_effects=True, vmem_limit_bytes=28 * 2**20),
         )(q, k, v)
 

time: 39.2 us -> 37.7 us (0.962)
  the two profiles are of different devices: /device:TPU:22 before, /device:TPU:21 now
where the time goes in v3:
time: 37.7 us; the launch traced here: 37.6 us
  Pallas kernels  36.8 us (98%)
  local copies, waits for them, and re-layouts  0.8 us (2%)
    pallas_call x1, Pallas kernels, step(): pl.pallas_call(functools.partial(kernel, n), out_shape=jax.ShapeDtypeStru...  36.8 us
    unnamed x1, local copies, waits for them, and re-layouts  0.8 us

profile of v3, /device:TPU:21, one launch (start us, length us, event | category | flops | bytes accessed | tf_op | source)
XLA Modules:
  0.0 37.6 jit_solution(1178549762586959100)
XLA Ops:
  0.0 36.8 %shard_map.37 = bf16[32,64,64]{2,1,0:T(8,128)(2,1)S(1)} custom-call(bf16[32,64,64]{2,1,0:T(8,128)(2,1)} %q_ref.1, bf16[32,512,1024]{2,1,0:T(8,128)(2,1)} %bitcast.6, bf16[32,512,1024]{2,1,0:T(8,128)(2,1)} %bitcast.7), custom_call_target="tpu_custom_call" | custom-call | tf_op jit(solution)/shard_map/pallas_call | solution.py:300
  36.8 0.8 %copy.5 = bf16[32,64,64]{2,1,0:T(8,128)(2,1)} copy(bf16[32,64,64]{2,1,0:T(8,128)(2,1)S(1)} %shard_map.37) | data formatting | bytes 524288

commit v4 on v3

--- a/solution.py
+++ b/solution.py
@@ -11,7 +11,7 @@
 MESH = pl.DeviceIdType.MESH
 F32, BF16 = jnp.float32, jnp.bfloat16
 TILE = 256
-SLOTS = 8
+SLOTS = 6
 LAG = 3
 LATE = 2
 

time: 37.7 us -> 37.8 us (level)
  no operation moved by 1% of the time
where the time goes in v4:
time: 37.8 us
  Pallas kernels  37 us (98%)
  local copies, waits for them, and re-layouts  0.8 us (2%)
    pallas_call x1, Pallas kernels, step(): pl.pallas_call(functools.partial(kernel, n), out_shape=jax.ShapeDtypeStru...  37 us
    unnamed x1, local copies, waits for them, and re-layouts  0.8 us

profile of v4, /device:TPU:21, one launch (start us, length us, event | category | flops | bytes accessed | tf_op | source)
XLA Modules:
  0.0 37.8 jit_solution(13476293180532692269)
XLA Ops:
  0.0 37.0 %shard_map.37 = bf16[32,64,64]{2,1,0:T(8,128)(2,1)S(1)} custom-call(bf16[32,64,64]{2,1,0:T(8,128)(2,1)} %q_ref.1, bf16[32,512,1024]{2,1,0:T(8,128)(2,1)} %bitcast.6, bf16[32,512,1024]{2,1,0:T(8,128)(2,1)} %bitcast.7), custom_call_target="tpu_custom_call" | custom-call | tf_op jit(solution)/shard_map/pallas_call | solution.py:300
  37.0 0.8 %copy.5 = bf16[32,64,64]{2,1,0:T(8,128)(2,1)} copy(bf16[32,64,64]{2,1,0:T(8,128)(2,1)S(1)} %shard_map.37) | data formatting | bytes 524288
